TPU v7x, 256 devices: a whole 4x4x8 slice. The times are simulated.
256 devices in a mesh: site: 64 (over z_hi, x, y, core), vec: 4 (over z_lo).
Axes of the slice: x: 4, y: 4, z: 8 (z_hi: 2, z_lo: 4; z = z_hi * 4 + z_lo), core: 2. Of those that a mesh axis runs over, the one named last changes fastest.
Arguments:
- vector_signs: int32 [64, 1024, 2048], P('vec', 'site'), may hold values from 0 to 1
- disorder: int32 [1024, 2048], P('site'), may hold values from 0 to 7
- bond_types: int32 [2, 1024, 2048], P(None, 'site'), may hold values from 0 to 3
- onsite_table: float32 [8], replicated, may hold values from -2 to 2
- hop_table: float32 [4], replicated, may hold values from 0.5 to 1.5
Outputs:
- moments: float32 [4, 4, 16, 16], replicated
All inputs are finite; a program needn't handle non-finite values.
Results may differ from a plain program's by a relative error of at most 0.000075.
Values sent between devices are 32-bit elements; how exact they have to be, the bound alone decides.
A program may use at most 128 MiB of HBM per device.

v0:
```python
import functools

import jax
import jax.numpy as jnp
from jax import lax
from jax.experimental import pallas as pl
from jax.experimental.pallas import tpu as pltpu
from jax.sharding import PartitionSpec as P

MESH = pl.DeviceIdType.MESH
DEPTH = 4
SPLIT = (2, 4, 4, 2)
spectral_bound = 8.5
scale = 2.0 / spectral_bound


def rolled(v, shift):
    return pltpu.roll(v, shift % v.shape[1], 1)


def lookup(codes, table, count, factor):
    result = jnp.zeros(codes.shape, jnp.float32)
    for k in range(count):
        result = jnp.where(codes == k, table[k] * factor, result)
    return result


def kernel(
    dims,
    signs,
    disorder,
    bonds,
    onsite_table,
    hop_table,
    out,
    codes,
    fields,
    raw,
    base,
    right_1,
    right_2,
    right_3,
    left_0,
    left_1,
    left_2,
    lefts,
    drifts,
    acc,
    packed,
    core_in,
    y_buf,
    x_buf,
    z_buf,
    final,
    row_sem,
    code_sem,
    row_send,
    row_recv,
    code_send,
    code_recv,
    red_send,
    red_recv,
):
    n_hi, n_x, n_y, n_core, n_lo = dims
    n_site = n_hi * n_x * n_y * n_core
    n_z = n_hi * n_lo
    rows = signs.shape[1]
    total = rows + 2 * DEPTH
    cols = signs.shape[2]
    half_rows = 8
    site = lax.axis_index("site")
    vec = lax.axis_index("vec")
    core = lax.rem(site, n_core)
    y = lax.rem(site // n_core, n_y)
    x = lax.rem(site // (n_core * n_y), n_x)
    z = (site // (n_core * n_y * n_x)) * n_lo + vec

    def device(xx, yy, zz):
        return (
            (zz // n_lo) * (n_x * n_y * n_core) + xx * (n_y * n_core) + yy * n_core + core,
            lax.rem(zz, n_lo),
        )

    partner = (site + 1 - 2 * core, vec)
    across = (lax.rem(site + n_site + 2 * core - 1, n_site), vec)
    y_peers = [device(x, lax.rem(y + k, n_y), z) for k in range(1, n_y)]
    x_peers = [device(lax.rem(x + k, n_x), y, z) for k in range(1, n_x)]
    z_peers = [device(x, y, lax.rem(z + k, n_z)) for k in range(1, n_z)]

    barrier = pltpu.get_barrier_semaphore()
    everyone = [partner, across, *y_peers, *x_peers, *z_peers]
    for peer in everyone:
        pl.semaphore_signal(barrier, inc=1, device_id=peer, device_id_type=MESH)

    def mine(k):
        return pltpu.make_async_copy(signs.at[:, k], raw.at[DEPTH + k], row_sem.at[k])

    def far_row(i):
        return core * (rows - 1 - i) + (1 - core) * i

    def near_row(i):
        return (1 - core) * (rows - 1 - i) + core * i

    for i in range(DEPTH):
        mine(near_row(i)).start()
    own_codes = [
        pltpu.make_async_copy(src, codes.at[j, pl.ds(0, rows)], code_sem.at[j])
        for j, src in enumerate((disorder, bonds.at[0], bonds.at[1]))
    ]
    for copy in own_codes:
        copy.start()
    for i in range(DEPTH):
        mine(far_row(i)).start()
    for i in range(DEPTH, rows - DEPTH):
        mine(i).start()

    def send_row(side, i):
        own = near_row(i) if side == 0 else far_row(i)
        flag = core if side == 0 else 1 - core
        there = flag * (DEPTH + rows + i) + (1 - flag) * (DEPTH - 1 - i)
        return pltpu.make_async_remote_copy(
            src_ref=raw.at[DEPTH + own],
            dst_ref=raw.at[there],
            send_sem=row_send.at[side, i],
            recv_sem=row_recv.at[side, i],
            device_id=partner if side == 0 else across,
            device_id_type=MESH,
        )

    def send_codes(side, upward, j):
        src = rows - DEPTH if upward else 0
        dst = rows + DEPTH if upward else rows
        return pltpu.make_async_remote_copy(
            src_ref=codes.at[j, pl.ds(src, DEPTH)],
            dst_ref=codes.at[j, pl.ds(dst, DEPTH)],
            send_sem=code_send.at[side, j],
            recv_sem=code_recv.at[side, j],
            device_id=partner if side == 0 else across,
            device_id_type=MESH,
        )

    pl.semaphore_wait(barrier, len(everyone))
    for i in range(DEPTH):
        mine(near_row(i)).wait()
        send_row(0, i).start()
    for copy in own_codes:
        copy.wait()

    @pl.when(core == 1)
    def _():
        for j in range(3):
            send_codes(0, False, j).start()
            send_codes(1, True, j).start()

    @pl.when(core == 0)
    def _():
        for j in range(3):
            send_codes(0, True, j).start()
            send_codes(1, False, j).start()

    for i in range(DEPTH):
        mine(far_row(i)).wait()
        send_row(1, i).start()
    for i in range(DEPTH, rows - DEPTH):
        mine(i).wait()

    def decode(start, size):
        at = pl.ds(start, size)
        fields[0, at, :] = lookup(codes[0, at, :], onsite_table, onsite_table.shape[0], scale)
        fields[1, at, :] = lookup(codes[1, at, :], hop_table, hop_table.shape[0], -scale)
        fields[2, at, :] = lookup(codes[2, at, :], hop_table, hop_table.shape[0], -scale)

    def decode_side(side):
        upper = side == 1
        for j in range(3):
            send_codes(side, True, j).wait_recv()

        @pl.when(core == 1)
        def _():
            decode(rows if upper else rows + DEPTH, DEPTH)

        @pl.when(core == 0)
        def _():
            decode(rows + DEPTH if upper else rows, DEPTH)

    for start in range(0, rows, 8):
        decode(start, 8)
    decode_side(0)
    for i in range(DEPTH):
        send_row(0, i).wait_recv()

    def natural(s):
        return core * s + (1 - core) * (total - 1 - s)

    def place(n):
        return lax.rem(n + total - DEPTH, total)

    def site_field(j, s):
        return jnp.broadcast_to(fields[j, pl.ds(place(natural(s)), 1), :], (half_rows, cols))

    def bond(s):
        n = core * s + (1 - core) * (total - 2 - s)
        return jnp.broadcast_to(fields[2, pl.ds(place(n), 1), :], (half_rows, cols))

    def keep(stack, order, s, h, v):
        high = v.astype(jnp.bfloat16).astype(jnp.float32)
        both = jnp.concatenate([high, v - high], axis=0).astype(jnp.bfloat16)
        at = pl.ds(pl.multiple_of(order * 32 + h * 16, 16), 16)
        if stack is None:
            lefts[lax.rem(s, 8), at, :] = both
            drifts[lax.rem(s, 8), at, :] = both
        else:
            stack[lax.rem(s, 8), at, :] = both

    def columns(v, s):
        hop = site_field(1, s)
        return site_field(0, s) * v + hop * rolled(v, -1) + rolled(hop * v, 1)

    def load_base(t, h):
        codes_now = raw[natural(t), pl.ds(pl.multiple_of(h * 8, 8), 8), :]
        value = jnp.where(codes_now == 1, 1.0, -1.0).astype(jnp.float32)
        base[t, h] = value
        return value

    def advance(u, levels):
        t = u // 2
        h = lax.rem(u, 2)
        ahead = load_base(t, h)
        if levels >= 1:
            s = t - 1
            forth, back = bond(s) * ahead, bond(s - 1) * base[s - 1, h]
            left_new = forth - back
            left_0[s, h] = left_new
            keep(None, 0, s, h, left_new)
            right_new = columns(base[s, h], s) + (forth + back)
            right_1[s, h] = right_new
        if levels >= 2:
            s = t - 2
            up, down = bond(s), bond(s - 1)
            forth, back = up * right_new, down * right_1[s - 1, h]
            keep(drifts, 1, s, h, forth - back)
            twice = base[s, h]
            right_new = columns(right_1[s, h], s) + (forth + back) - (twice + twice)
            right_2[s, h] = right_new
            left_new = columns(left_0[s, h], s) + (up * left_new + down * left_0[s - 1, h])
            left_1[s, h] = left_new
            keep(lefts, 1, s, h, left_new)
        if levels >= 3:
            s = t - 3
            up, down = bond(s), bond(s - 1)
            forth, back = up * right_new, down * right_2[s - 1, h]
            keep(drifts, 2, s, h, forth - back)
            right_new = columns(right_2[s, h], s) + (forth + back) - right_1[s, h]
            right_3[s, h] = right_new
            twice = left_0[s, h]
            left_new = columns(left_1[s, h], s) + (up * left_new + down * left_1[s - 1, h]) - (twice + twice)
            left_2[s, h] = left_new
            keep(lefts, 2, s, h, left_new)
        if levels >= 4:
            s = t - 4
            up, down = bond(s), bond(s - 1)
            keep(drifts, 3, s, h, up * right_new - down * right_3[s - 1, h])
            left_new = columns(left_2[s, h], s) + (up * left_new + down * left_2[s - 1, h]) - left_1[s, h]
            keep(lefts, 3, s, h, left_new)

    width = cols // 2

    def multiply(s, h):
        slot = lax.rem(s, 8)
        at = pl.ds(pl.multiple_of(h * width, 128), width)
        acc[...] += lax.dot_general(
            lefts[slot, :, at],
            drifts[slot, :, at],
            (((1,), (1,)), ((), ())),
            preferred_element_type=jnp.float32,
        )

    for levels in range(4):
        first = 0 if levels == 0 else 2 * levels

        def warm(u, carry, levels=levels):
            advance(u, levels)
            return carry

        lax.fori_loop(2 * first, 2 * (2 * levels + 2), warm, 0)

    first_full = 2 * DEPTH

    def full(u, carry):
        t = u // 2

        @pl.when(u == 2 * (rows + DEPTH))
        def _():
            decode_side(1)

        @pl.when(jnp.logical_and(t >= rows + DEPTH, lax.rem(u, 2) == 0))
        def _():
            i = t - (rows + DEPTH)
            pltpu.make_async_copy(signs.at[:, 0], raw.at[0], row_recv.at[1, i]).wait()

        multiply(t - 5, lax.rem(u, 2))

        @pl.when(u == 2 * first_full + 1)
        def _():
            acc[...] = jnp.zeros_like(acc)

        advance(u, 4)
        return carry

    lax.fori_loop(2 * first_full, 2 * total, full, 0)
    for h in range(2):
        multiply(total - 1 - DEPTH, h)

    whole = jnp.concatenate([acc[16 * b : 16 * b + 8, :] + acc[16 * b + 8 : 16 * b + 16, :] for b in range(8)], axis=0)
    whole = whole + rolled(whole, -8)
    lane = lax.broadcasted_iota(jnp.int32, (32, 128), 1)
    packed[...] = jnp.where((lane // 8) % 2 == 0, whole[:32], rolled(whole[32:], 8)).reshape(2, 16, 128)

    def send(src, dst, k, peer):
        return pltpu.make_async_remote_copy(
            src_ref=src, dst_ref=dst, send_sem=red_send.at[k], recv_sem=red_recv.at[k], device_id=peer, device_id_type=MESH
        )

    first = send(packed.at[1 - core], core_in, 0, partner)
    first.start()
    first.wait_recv()
    value = packed[core] + core_in[...]
    waits = [first]
    start = 1
    for buf, place_now, peers, size in ((y_buf, y, y_peers, n_y), (x_buf, x, x_peers, n_x), (z_buf, z, z_peers, n_z)):
        buf[place_now] = value
        for k, peer in enumerate(peers):
            copy = pltpu.make_async_remote_copy(
                src_ref=buf.at[place_now],
                dst_ref=buf.at[place_now],
                send_sem=red_send.at[start + k],
                recv_sem=red_recv.at[start + k],
                device_id=peer,
                device_id_type=MESH,
            )
            copy.start()
            waits.append(copy)
        for k in range(size - 1):
            waits[start + k].wait_recv()
        value = buf[0]
        for k in range(1, size):
            value = value + buf[k]
        start += size - 1
    final[core] = value
    last = send(final.at[core], final.at[core], start, partner)
    last.start()
    last.wait_recv()
    waits.append(last)

    done = final[...].reshape(32, 128)
    lane = lax.broadcasted_iota(jnp.int32, (16, 128), 1)
    per_site = -1.0 / (n_site * rows * cols * n_lo) / (scale * scale)
    for p in range(4):
        strip = done[(p % 2) * 16 : (p % 2) * 16 + 16]
        for q in range(4):
            at = q * 32 + (p // 2) * 8
            block = jnp.where(lane < 8, rolled(strip, -at), rolled(strip, -at - 8))
            factor = per_site * (0.5 if p else 1.0) * (0.5 if q else 1.0)
            out[p, q] = block[:, :16] * factor

    for copy in waits:
        copy.wait_send()
    for side in range(2):
        for i in range(DEPTH):
            send_row(side, i).wait_send()
        for j in range(3):
            send_codes(side, True, j).wait_send()


def solution(mesh):
    n_hi, n_x, n_y, n_core = SPLIT
    n_lo = mesh.shape["vec"]
    dims = (mesh.shape["site"] // (n_x * n_y * n_core), n_x, n_y, n_core, n_lo)

    def shards(vector_signs, disorder, bond_types, onsite_table, hop_table):
        width, rows, cols = vector_signs.shape
        total = rows + 2 * DEPTH
        n_red = 2 + (n_y - 1) + (n_x - 1) + (dims[0] * n_lo - 1)
        full = pltpu.VMEM((total, 2, 8, cols), jnp.float32)
        anywhere = pl.BlockSpec(memory_space=pl.ANY)
        scalars = pl.BlockSpec(memory_space=pltpu.SMEM)
        return pl.pallas_call(
            functools.partial(kernel, dims),
            out_shape=jax.ShapeDtypeStruct((4, 4, width, width), jnp.float32),
            in_specs=[anywhere, anywhere, anywhere, scalars, scalars],
            out_specs=pl.BlockSpec(memory_space=pltpu.VMEM),
            scratch_shapes=[
                pltpu.VMEM((3, total, cols), jnp.int32),
                pltpu.VMEM((3, total, cols), jnp.float32),
                pltpu.VMEM((total, width, cols), jnp.int32),
                full,
                full,
                full,
                full,
                full,
                full,
                full,
                pltpu.VMEM((8, 128, cols), jnp.bfloat16),
                pltpu.VMEM((8, 128, cols), jnp.bfloat16),
                pltpu.VMEM((128, 128), jnp.float32),
                pltpu.VMEM((2, 16, 128), jnp.float32),
                pltpu.VMEM((16, 128), jnp.float32),
                pltpu.VMEM((n_y, 16, 128), jnp.float32),
                pltpu.VMEM((n_x, 16, 128), jnp.float32),
                pltpu.VMEM((dims[0] * n_lo, 16, 128), jnp.float32),
                pltpu.VMEM((2, 16, 128), jnp.float32),
                pltpu.SemaphoreType.DMA((rows,)),
                pltpu.SemaphoreType.DMA((3,)),
                pltpu.SemaphoreType.DMA((2, DEPTH)),
                pltpu.SemaphoreType.DMA((2, DEPTH)),
                pltpu.SemaphoreType.DMA((2, 3)),
                pltpu.SemaphoreType.DMA((2, 3)),
                pltpu.SemaphoreType.DMA((n_red,)),
                pltpu.SemaphoreType.DMA((n_red,)),
            ],
            compiler_params=pltpu.CompilerParams(
                collective_id=0, has_side_effects=True, vmem_limit_bytes=60 * 1024 * 1024
            ),
        )(vector_signs, disorder, bond_types, onsite_table, hop_table)

    return jax.shard_map(
        shards,
        mesh=mesh,
        in_specs=(P("vec", "site", None), P("site", None), P(None, "site", None), P(), P()),
        out_specs=P(),
        check_vma=False,
    )
```

profile of v0, /device:TPU:1, one launch (start us, length us, event | category | flops | bytes accessed | tf_op | source)
XLA Modules:
  0.0 57.1 jit_solution(16323389985033797296)
XLA Ops:
  0.0 55.5 %shard_map.55 = f32[4,4,16,16]{3,2,1,0:T(8,128)} custom-call(s32[16,16,2048]{2,1,0:T(8,128)} %signs.1, s32[16,2048]{1,0:T(8,128)} %disorder.1, s32[2,16,2048]{2,1,0:T(8,128)} %bonds.1, f32[8]{0:T(128)} %onsite_table.1, f32[4]{0:T(128)} %hop_table.1), custom_call_target="tpu_custom_call" | custom-call | tf_op jit(solution)/shard_map/pallas_call | solution.py:387
  55.5 1.6 %copy.7 = f32[4,4,16,16]{3,2,1,0:T(8,128)} copy(f32[4,4,16,16]{3,2,1,0:T(8,128)} %shard_map.55) | data formatting | bytes 32768
where the time goes:
time: 57.2 us; the launch traced here: 57.1 us
  Pallas kernels  55.5 us (97%)
  local copies, waits for them, and re-layouts  1.57 us (3%)
    pallas_call x1, Pallas kernels, shards(): pl.pallas_call(functools.partial(kernel, dims), out_shape=jax.ShapeDtypeS...  55.5 us
    unnamed x1, local copies, waits for them, and re-layouts  1.57 us

commit v1 on v0

v1 whole, which is shorter than its diff:
```python
import functools

import jax
import jax.numpy as jnp
from jax import lax
from jax.experimental import pallas as pl
from jax.experimental.pallas import tpu as pltpu
from jax.sharding import PartitionSpec as P

MESH = pl.DeviceIdType.MESH
DEPTH = 4
WIDTH = 2048
CHUNK = 256
EXCHANGE_AT = 2
RELAY_AT = 13
SPLIT = (2, 4, 4, 2)
spectral_bound = 8.5
scale = 2.0 / spectral_bound


def rolled(v, shift):
    return pltpu.roll(v, shift % v.shape[1], 1)


def lookup(codes, table, count, factor):
    result = jnp.zeros(codes.shape, jnp.float32)
    for k in range(count):
        result = jnp.where(codes == k, table[k] * factor, result)
    return result


def kernel(
    dims,
    signs,
    disorder,
    bonds,
    onsite_table,
    hop_table,
    out,
    codes,
    fields,
    bonds_y,
    raw,
    relay_buf,
    relay_codes,
    base,
    right_1,
    right_2,
    right_3,
    left_0,
    left_1,
    left_2,
    left_3,
    drift_1,
    drift_2,
    drift_3,
    acc,
    packed,
    core_in,
    plane_buf,
    z_buf,
    final,
    row_sem,
    code_sem,
    row_send,
    row_recv,
    code_send,
    code_recv,
    relay_sem,
    red_send,
    red_recv,
):
    n_hi, n_x, n_y, n_core, n_lo = dims
    n_site = n_hi * n_x * n_y * n_core
    n_z = n_hi * n_lo
    rows = signs.shape[1]
    total = rows + 2 * DEPTH
    cols = signs.shape[2]
    site = lax.axis_index("site")
    vec = lax.axis_index("vec")
    core = lax.rem(site, n_core)
    y = lax.rem(site // n_core, n_y)
    x = lax.rem(site // (n_core * n_y), n_x)
    z = (site // (n_core * n_y * n_x)) * n_lo + vec

    def device(xx, yy, zz, cc):
        return (
            (zz // n_lo) * (n_x * n_y * n_core) + xx * (n_y * n_core) + yy * n_core + cc,
            lax.rem(zz, n_lo),
        )

    def is_last(xx, yy):
        return (xx // (n_x - 1)) * (yy // (n_y - 1))

    def around(k):
        return lax.rem(z + k + n_z, n_z)

    partner = (site + 1 - 2 * core, vec)
    across = (lax.rem(site + n_site + 2 * core - 1, n_site), vec)
    summing = core == 1 - is_last(x, y)
    plane_peers = []
    for j in range(n_x):
        for k in range(n_y):
            if j or k:
                xx, yy = lax.rem(x + j, n_x), lax.rem(y + k, n_y)
                plane_peers.append(device(xx, yy, z, 1 - is_last(xx, yy)))
    z_peers = [device(x, y, around(k), core) for k in range(1, n_z)]

    def count(flag):
        return flag.astype(jnp.int32)

    mirror_x = core * x + (1 - core) * (n_x - 1 - x)
    mirror_y = core * y + (1 - core) * (n_y - 1 - y)
    crossing = jnp.logical_and(mirror_x == n_x - 1, mirror_y == n_y - 1)
    by_end = jnp.logical_and(mirror_x == 0, mirror_y == n_y - 1)
    by_next = jnp.logical_and(mirror_x == n_x - 2, mirror_y == n_y - 1)
    by_z = jnp.logical_and(mirror_x == 0, mirror_y == 0)
    by_x = jnp.logical_or(by_end, by_next)
    relaying = jnp.logical_or(by_x, by_z)
    plane = n_x * n_y * n_core
    half = n_z // 2
    far_x, far_y = core * (n_x - 1), core * (n_y - 1)
    near_x, near_y = (1 - core) * (n_x - 1), (1 - core) * (n_y - 1)
    next_x = core * (n_x - 2) + (1 - core)
    source_core = core + count(by_z) * (1 - 2 * core)

    def relay_of(i):
        if i == 0:
            return device(near_x, far_y, z, core)
        if i == 2:
            return device(next_x, far_y, z, core)
        return device(far_x, far_y, around(i - 2), 1 - core)

    def relay_to(k):
        zz = around(half + count(by_z)) if k == 0 else around(half - 1)
        return ((zz // n_lo) * plane + (1 - source_core) * (plane - 1), lax.rem(zz, n_lo))

    barrier = pltpu.get_barrier_semaphore()

    def greet(peers):
        for peer in peers:
            pl.semaphore_signal(barrier, inc=1, device_id=peer, device_id_type=MESH)

    @pl.when(by_x)
    def _():
        greet([device(far_x, far_y, z, core)])

    @pl.when(by_z)
    def _():
        greet([device(x, y, around(k), 1 - core) for k in (1, -1)])

    @pl.when(crossing)
    def _():
        other_next = (1 - core) * (n_x - 2) + core
        greet(
            [
                device(far_x, near_y, around(half), 1 - core),
                device(other_next, near_y, around(half), 1 - core),
                device(near_x, near_y, around(half - 1), core),
                device(near_x, near_y, around(half + 1), core),
            ]
        )

    greet([partner])

    @pl.when(jnp.logical_not(crossing))
    def _():
        greet([across])

    @pl.when(summing)
    def _():
        greet(plane_peers + z_peers)

    n_greeted = (
        2 + count(summing) * (len(plane_peers) + len(z_peers)) + 3 * count(crossing) + count(by_x) + 2 * count(by_z)
    )

    def mine(k):
        return pltpu.make_async_copy(signs.at[:, k], raw.at[DEPTH + k], row_sem.at[k])

    def far_row(i):
        return core * (rows - 1 - i) + (1 - core) * i

    def near_row(i):
        return (1 - core) * (rows - 1 - i) + core * i

    for i in range(DEPTH):
        mine(far_row(i)).start()
    own_codes = [
        pltpu.make_async_copy(src, codes.at[j, pl.ds(0, rows)], code_sem.at[j])
        for j, src in enumerate((disorder, bonds.at[0], bonds.at[1]))
    ]
    for copy in own_codes:
        copy.start()
    for i in range(DEPTH):
        mine(near_row(i)).start()
    for i in range(DEPTH, rows - DEPTH):
        mine(i).start()

    def place(n):
        return lax.rem(n + total - DEPTH, total)

    def landing(side, i, source=None):
        flag = core if side == 0 else 1 - (core if source is None else source)
        return flag * (DEPTH + rows + i) + (1 - flag) * (DEPTH - 1 - i)

    def send_row(side, i, by_relay=False):
        own = near_row(i) if side == 0 else far_row(i)
        return pltpu.make_async_remote_copy(
            src_ref=raw.at[DEPTH + own],
            dst_ref=relay_buf.at[i // 3] if by_relay else raw.at[landing(side, i)],
            send_sem=row_send.at[side, i],
            recv_sem=relay_sem.at[0, i // 3] if by_relay else row_recv.at[side, i],
            device_id=relay_of(i) if by_relay else (partner if side == 0 else across),
            device_id_type=MESH,
        )

    def send_far_codes(i, by_relay=False):
        return pltpu.make_async_remote_copy(
            src_ref=codes.at[:, far_row(i)],
            dst_ref=relay_codes.at[:, i // 3] if by_relay else codes.at[:, place(landing(1, i))],
            send_sem=code_send.at[1, i],
            recv_sem=relay_sem.at[1, i // 3] if by_relay else code_recv.at[1, i],
            device_id=relay_of(i) if by_relay else across,
            device_id_type=MESH,
        )

    def relays(k):
        i = count(by_z) + 2 * count(by_next) if k == 0 else 3
        n = landing(1, i, source_core)
        return [
            pltpu.make_async_remote_copy(
                src_ref=src, dst_ref=dst, send_sem=relay_sem.at[2 + j, k], recv_sem=sem.at[1, i], device_id=relay_to(k), device_id_type=MESH
            )
            for j, (src, dst, sem) in enumerate(
                ((relay_buf.at[k], raw.at[n], row_recv), (relay_codes.at[:, k], codes.at[:, place(n)], code_recv))
            )
        ]

    def relay_on(k):
        row, code = relays(k)
        pltpu.make_async_copy(codes.at[:, 0], relay_codes.at[:, k], relay_sem.at[1, k]).wait()
        code.start()
        pltpu.make_async_copy(signs.at[:, 0], relay_buf.at[k], relay_sem.at[0, k]).wait()
        row.start()

    def send_codes(upward, j):
        src = rows - DEPTH if upward else 0
        dst = rows + DEPTH if upward else rows
        return pltpu.make_async_remote_copy(
            src_ref=codes.at[j, pl.ds(src, DEPTH)],
            dst_ref=codes.at[j, pl.ds(dst, DEPTH)],
            send_sem=code_send.at[0, j],
            recv_sem=code_recv.at[0, j],
            device_id=partner,
            device_id_type=MESH,
        )

    def exchange():
        pl.semaphore_wait(barrier, n_greeted)
        for i in range(DEPTH):

            @pl.when(crossing)
            def _(i=i):
                send_row(1, i, True).start()
                send_far_codes(i, True).start()

            @pl.when(jnp.logical_not(crossing))
            def _(i=i):
                send_row(1, i).start()
                send_far_codes(i).start()

        @pl.when(core == 1)
        def _():
            for j in range(3):
                send_codes(False, j).start()

        @pl.when(core == 0)
        def _():
            for j in range(3):
                send_codes(True, j).start()

        for i in range(DEPTH):
            send_row(0, i).start()

    def decode(start, size, first):
        at = pl.ds(start, size)
        onsite = lookup(codes[0, at, :], onsite_table, onsite_table.shape[0], scale)
        hop_x = lookup(codes[1, at, :], hop_table, hop_table.shape[0], -scale)
        hop_y = lookup(codes[2, at, :], hop_table, hop_table.shape[0], -scale)
        hop_back = rolled(hop_x, 1)
        for i in range(size):
            n = first + i
            s = core * n + (1 - core) * (total - 1 - n)
            for j, value in enumerate((onsite, hop_x, hop_back)):
                fields[j, s] = jnp.broadcast_to(value[i : i + 1], (8, cols))
            bonds_y[core * (n + 1) + (1 - core) * (total - 1 - n)] = jnp.broadcast_to(hop_y[i : i + 1], (8, cols))

    def decode_side(side):
        upper = side == 1
        if side == 0:
            for j in range(3):
                send_codes(True, j).wait_recv()
        else:
            for i in range(DEPTH):
                send_far_codes(i).wait_recv()

        @pl.when(core == 1)
        def _():
            decode(rows if upper else rows + DEPTH, DEPTH, rows + DEPTH if upper else 0)

        @pl.when(core == 0)
        def _():
            decode(rows + DEPTH if upper else rows, DEPTH, 0 if upper else rows + DEPTH)

    for copy in own_codes:
        copy.wait()
    for start in range(0, rows, 8):
        decode(start, 8, DEPTH + start)
    for i in range(rows):
        mine(i).wait()

    def natural(s):
        return core * s + (1 - core) * (total - 1 - s)

    def split(v):
        high = v.astype(jnp.bfloat16).astype(jnp.float32)
        return jnp.concatenate([high, v - high], axis=0).astype(jnp.bfloat16)

    def advance(t, levels, step=1):
        for lo in range(0, cols, WIDTH):
            here = pl.ds(lo, WIDTH)
            right = pl.ds((lo + WIDTH) % cols, 128)
            left = pl.ds((lo - 128) % cols, 128)

            def wide(v):
                return jnp.concatenate([v, v], axis=0)

            def bond(s):
                return wide(bonds_y[s + 1, :, here])

            def columns(ref, v, s):
                ext = jnp.concatenate([ref[s, :, left], v, ref[s, :, right]], axis=1)
                following = rolled(ext, -1)[:, 128 : 128 + WIDTH]
                previous = rolled(ext, 1)[:, 128 : 128 + WIDTH]
                return wide(fields[0, s, :, here]) * v + wide(fields[1, s, :, here]) * following + wide(fields[2, s, :, here]) * previous

            def toward(s):
                return (bond(s), bond(s - 1)) if step == 1 else (bond(s - 1), bond(s))

            def minus(u, v):
                return u - v if step == 1 else v - u

            ahead = jnp.where(raw[natural(t), :, here] == 1, 1.0, -1.0).astype(jnp.float32)
            base[t, :, here] = ahead
            if levels >= 1:
                s = t - step
                up, down = toward(s)
                forth, back = up * ahead, down * base[s - step, :, here]
                left_new = minus(forth, back)
                left_0[s, :, here] = left_new
                right_new = columns(base, base[s, :, here], s) + (forth + back)
                right_1[s, :, here] = right_new
            if levels >= 2:
                s = t - 2 * step
                up, down = toward(s)
                forth, back = up * right_new, down * right_1[s - step, :, here]
                drift_1[s, :, here] = minus(forth, back)
                twice = base[s, :, here]
                right_new = columns(right_1, right_1[s, :, here], s) + (forth + back) - (twice + twice)
                right_2[s, :, here] = right_new
                left_new = columns(left_0, left_0[s, :, here], s) + (up * left_new + down * left_0[s - step, :, here])
                left_1[s, :, here] = left_new
            if levels >= 3:
                s = t - 3 * step
                up, down = toward(s)
                forth, back = up * right_new, down * right_2[s - step, :, here]
                drift_2[s, :, here] = minus(forth, back)
                right_new = columns(right_2, right_2[s, :, here], s) + (forth + back) - right_1[s, :, here]
                right_3[s, :, here] = right_new
                twice = left_0[s, :, here]
                left_new = columns(left_1, left_1[s, :, here], s) + (up * left_new + down * left_1[s - step, :, here]) - (twice + twice)
                left_2[s, :, here] = left_new
            if levels >= 4:
                s = t - 4 * step
                up, down = toward(s)
                drift_3[s, :, here] = minus(up * right_new, down * right_3[s - step, :, here])
                left_new = columns(left_2, left_2[s, :, here], s) + (up * left_new + down * left_2[s - step, :, here]) - left_1[s, :, here]
                left_3[s, :, here] = left_new

    def multiply(s):
        product = None
        for lo in range(0, cols, CHUNK):
            here = pl.ds(lo, CHUNK)
            order_0 = split(left_0[s, :, here])
            lefts = jnp.concatenate([order_0] + [split(ref[s, :, here]) for ref in (left_1, left_2, left_3)], axis=0)
            drifts = jnp.concatenate([order_0] + [split(ref[s, :, here]) for ref in (drift_1, drift_2, drift_3)], axis=0)
            part = lax.dot_general(lefts, drifts, (((1,), (1,)), ((), ())), preferred_element_type=jnp.float32)
            product = part if product is None else product + part
        acc[...] += product

    for levels in range(4):

        def warm(t, carry, levels=levels):
            advance(t, levels)
            return carry

        lax.fori_loop(DEPTH + 2 * levels, DEPTH + 2 * levels + 2, warm, 0)
        if levels == 0:
            pl.when(crossing)(exchange)
        if levels == EXCHANGE_AT:
            pl.when(jnp.logical_not(crossing))(exchange)

    first = 3 * DEPTH

    def inner(t, carry):
        @pl.when(t == first + 1)
        def _():
            acc[...] = jnp.zeros_like(acc)

        @pl.when(jnp.logical_and(relaying, t == RELAY_AT))
        def _():
            relay_on(0)

        @pl.when(jnp.logical_and(by_z, t == RELAY_AT))
        def _():
            relay_on(1)

        multiply(t - DEPTH - 1)
        advance(t, 4)
        return carry

    lax.fori_loop(first, rows + DEPTH, inner, 0)

    decode_side(0)
    for i in range(DEPTH):
        send_row(0, i).wait_recv()

    def near(k, carry):
        t = DEPTH - 1 - k
        multiply(t + DEPTH + 1 + (rows - 1 - 2 * DEPTH) * (t // (DEPTH - 1)))
        advance(t, 4, -1)
        return carry

    lax.fori_loop(0, DEPTH, near, 0)

    decode_side(1)

    def far(t, carry):
        pltpu.make_async_copy(signs.at[:, 0], raw.at[0], row_recv.at[1, t - (rows + DEPTH)]).wait()
        multiply(t - DEPTH - 1 - (rows - 1 - DEPTH) * ((total - 1 - t) // (DEPTH - 1)))
        advance(t, 4)
        return carry

    lax.fori_loop(rows + DEPTH, total, far, 0)
    multiply(total - DEPTH - 1)

    whole = jnp.concatenate([acc[32 * b : 32 * b + 16, :] + acc[32 * b + 16 : 32 * b + 32, :] for b in range(4)], axis=0)
    whole = whole + rolled(whole, -16)
    lane = lax.broadcasted_iota(jnp.int32, (32, 128), 1)
    packed[...] = jnp.where((lane // 16) % 2 == 0, whole[:32], rolled(whole[32:], 16)).reshape(2, 16, 128)

    def send(src, dst, k, peer):
        return pltpu.make_async_remote_copy(
            src_ref=src, dst_ref=dst, send_sem=red_send.at[k], recv_sem=red_recv.at[k], device_id=peer, device_id_type=MESH
        )

    give = send(packed, core_in, 0, partner)
    take = send(final, final, 1, partner)

    @pl.when(summing)
    def _():
        give.wait_recv()
        halves = [packed[k] + core_in[k] for k in range(2)]
        waits = []
        start = 2
        places = (x * n_y + y, z)
        groups = (plane_peers, z_peers)
        for step in range(2):
            now = []
            for k in range(2):
                axis = (step + k) % 2
                buf = (plane_buf, z_buf)[axis].at[step]
                buf[places[axis]] = halves[k]
                for peer in groups[axis]:
                    now.append(send(buf.at[places[axis]], buf.at[places[axis]], start, peer))
                    now[-1].start()
                    start += 1
            for copy in now:
                copy.wait_recv()
            waits += now
            for k in range(2):
                axis = (step + k) % 2
                buf = (plane_buf, z_buf)[axis].at[step]
                value = buf[0]
                for j in range(1, len(groups[axis]) + 1):
                    value = value + buf[j]
                halves[k] = value
        for k in range(2):
            final[k] = halves[k]
        take.start()
        for copy in waits:
            copy.wait_send()

    @pl.when(jnp.logical_not(summing))
    def _():
        give.start()
        take.wait_recv()

    done = final[...].reshape(32, 128)
    per_site = -1.0 / (n_site * rows * cols * n_lo) / (scale * scale)
    for p in range(4):
        strip = done[(p % 2) * 16 : (p % 2) * 16 + 16]
        for q in range(4):
            block = rolled(strip, -(q * 32 + (p // 2) * 16))
            factor = per_site * (0.5 if p else 1.0) * (0.5 if q else 1.0)
            out[p, q] = block[:, :16] * factor

    @pl.when(summing)
    def _():
        take.wait_send()

    @pl.when(jnp.logical_not(summing))
    def _():
        give.wait_send()

    @pl.when(relaying)
    def _():
        for copy in relays(0):
            copy.wait_send()

    @pl.when(by_z)
    def _():
        for copy in relays(1):
            copy.wait_send()

    for side in range(2):
        for i in range(DEPTH):
            send_row(side, i).wait_send()
    for j in range(3):
        send_codes(True, j).wait_send()
    for i in range(DEPTH):
        send_far_codes(i).wait_send()


def solution(mesh):
    n_hi, n_x, n_y, n_core = SPLIT
    n_lo = mesh.shape["vec"]
    dims = (mesh.shape["site"] // (n_x * n_y * n_core), n_x, n_y, n_core, n_lo)

    def shards(vector_signs, disorder, bond_types, onsite_table, hop_table):
        width, rows, cols = vector_signs.shape
        total = rows + 2 * DEPTH
        n_z = dims[0] * n_lo
        n_red = 2 + 2 * (n_x * n_y - 1) + 2 * (n_z - 1)
        full = pltpu.VMEM((total, width, cols), jnp.float32)
        anywhere = pl.BlockSpec(memory_space=pl.ANY)
        scalars = pl.BlockSpec(memory_space=pltpu.SMEM)
        return pl.pallas_call(
            functools.partial(kernel, dims),
            out_shape=jax.ShapeDtypeStruct((4, 4, width, width), jnp.float32),
            in_specs=[anywhere, anywhere, anywhere, scalars, scalars],
            out_specs=pl.BlockSpec(memory_space=pltpu.VMEM),
            scratch_shapes=[
                pltpu.VMEM((3, total, cols), jnp.int32),
                pltpu.VMEM((3, total, 8, cols), jnp.float32),
                pltpu.VMEM((total + 1, 8, cols), jnp.float32),
                pltpu.VMEM((total, width, cols), jnp.int32),
                pltpu.VMEM((2, width, cols), jnp.int32),
                pltpu.VMEM((3, 2, cols), jnp.int32),
                full,
                full,
                full,
                full,
                full,
                full,
                full,
                full,
                full,
                full,
                full,
                pltpu.VMEM((128, 128), jnp.float32),
                pltpu.VMEM((2, 16, 128), jnp.float32),
                pltpu.VMEM((2, 16, 128), jnp.float32),
                pltpu.VMEM((2, n_x * n_y, 16, 128), jnp.float32),
                pltpu.VMEM((2, n_z, 16, 128), jnp.float32),
                pltpu.VMEM((2, 16, 128), jnp.float32),
                pltpu.SemaphoreType.DMA((rows,)),
                pltpu.SemaphoreType.DMA((3,)),
                pltpu.SemaphoreType.DMA((2, DEPTH)),
                pltpu.SemaphoreType.DMA((2, DEPTH)),
                pltpu.SemaphoreType.DMA((2, DEPTH)),
                pltpu.SemaphoreType.DMA((2, DEPTH)),
                pltpu.SemaphoreType.DMA((4, 2)),
                pltpu.SemaphoreType.DMA((n_red,)),
                pltpu.SemaphoreType.DMA((n_red,)),
            ],
            compiler_params=pltpu.CompilerParams(
                collective_id=0, has_side_effects=True, vmem_limit_bytes=60 * 1024 * 1024
            ),
        )(vector_signs, disorder, bond_types, onsite_table, hop_table)

    return jax.shard_map(
        shards,
        mesh=mesh,
        in_specs=(P("vec", "site", None), P("site", None), P(None, "site", None), P(), P()),
        out_specs=P(),
        check_vma=False,
    )
```

time: 57.2 us -> 44 us (0.77)
  Pallas kernels: 55.5 us -> 42.3 us
    pallas_call x1, Pallas kernels: 55.5 us -> 42.3 us  [shards(): pl.pallas_call(functools.partial(kernel, dims), out_shape=jax.ShapeDtypeS...]
where the time goes in v1:
time: 44 us; the launch traced here: 43.9 us
  Pallas kernels  42.3 us (96%)
  local copies, waits for them, and re-layouts  1.57 us (4%)
    pallas_call x1, Pallas kernels, shards(): pl.pallas_call(functools.partial(kernel, dims), out_shape=jax.ShapeDtypeS...  42.3 us
    unnamed x1, local copies, waits for them, and re-layouts  1.57 us

profile of v1, /device:TPU:1, one launch (start us, length us, event | category | flops | bytes accessed | tf_op | source)
XLA Modules:
  0.0 43.9 jit_solution(17009443266564314951)
XLA Ops:
  0.0 42.3 %shard_map.55 = f32[4,4,16,16]{3,2,1,0:T(8,128)} custom-call(s32[16,16,2048]{2,1,0:T(8,128)} %signs.1, s32[16,2048]{1,0:T(8,128)} %disorder.1, s32[2,16,2048]{2,1,0:T(8,128)} %bonds.1, f32[8]{0:T(128)} %onsite_table.1, f32[4]{0:T(128)} %hop_table.1), custom_call_target="tpu_custom_call" | custom-call | tf_op jit(solution)/shard_map/pallas_call | solution.py:559
  42.3 1.6 %copy.7 = f32[4,4,16,16]{3,2,1,0:T(8,128)} copy(f32[4,4,16,16]{3,2,1,0:T(8,128)} %shard_map.55) | data formatting | bytes 32768

commit v2 on v1

--- a/solution.py
+++ b/solution.py
@@ -11,8 +11,8 @@
 DEPTH = 4
 WIDTH = 2048
 CHUNK = 256
-EXCHANGE_AT = 2
-RELAY_AT = 13
+EXCHANGE_AT = 3
+RELAY_AT = 14
 SPLIT = (2, 4, 4, 2)
 spectral_bound = 8.5
 scale = 2.0 / spectral_bound

time: 44 us -> 42.8 us (0.973)
  Pallas kernels: 42.3 us -> 41.1 us
    pallas_call x1, Pallas kernels: 42.3 us -> 41.1 us  [shards(): pl.pallas_call(functools.partial(kernel, dims), out_shape=jax.ShapeDtypeS...]
where the time goes in v2:
time: 42.8 us; the launch traced here: 42.7 us
  Pallas kernels  41.1 us (96%)
  local copies, waits for them, and re-layouts  1.57 us (4%)
    pallas_call x1, Pallas kernels, shards(): pl.pallas_call(functools.partial(kernel, dims), out_shape=jax.ShapeDtypeS...  41.1 us
    unnamed x1, local copies, waits for them, and re-layouts  1.57 us

profile of v2, /device:TPU:1, one launch (start us, length us, event | category | flops | bytes accessed | tf_op | source)
XLA Modules:
  0.0 42.7 jit_solution(17840831112272617078)
XLA Ops:
  0.0 41.1 %shard_map.55 = f32[4,4,16,16]{3,2,1,0:T(8,128)} custom-call(s32[16,16,2048]{2,1,0:T(8,128)} %signs.1, s32[16,2048]{1,0:T(8,128)} %disorder.1, s32[2,16,2048]{2,1,0:T(8,128)} %bonds.1, f32[8]{0:T(128)} %onsite_table.1, f32[4]{0:T(128)} %hop_table.1), custom_call_target="tpu_custom_call" | custom-call | tf_op jit(solution)/shard_map/pallas_call | solution.py:559
  41.1 1.6 %copy.7 = f32[4,4,16,16]{3,2,1,0:T(8,128)} copy(f32[4,4,16,16]{3,2,1,0:T(8,128)} %shard_map.55) | data formatting | bytes 32768

commit v3 on v2

--- a/solution.py
+++ b/solution.py
@@ -11,7 +11,7 @@
 DEPTH = 4
 WIDTH = 2048
 CHUNK = 256
-EXCHANGE_AT = 3
+EXCHANGE_AT = 1
 RELAY_AT = 14
 SPLIT = (2, 4, 4, 2)
 spectral_bound = 8.5
@@ -67,6 +67,7 @@
     code_send,
     code_recv,
     relay_sem,
+    round_sem,
     red_send,
     red_recv,
 ):
@@ -106,6 +107,21 @@
                 plane_peers.append(device(xx, yy, z, 1 - is_last(xx, yy)))
     z_peers = [device(x, y, around(k), core) for k in range(1, n_z)]
 
+    next_chips = []
+    for j, k in ((1, 0), (n_x - 1, 0), (0, 1), (0, n_y - 1)):
+        xx, yy = lax.rem(x + j, n_x), lax.rem(y + k, n_y)
+        next_chips.append(device(xx, yy, z, 1 - is_last(xx, yy)))
+    next_chips += [device(x, y, around(k), core) for k in (1, -1)]
+
+    def pass_on(heard, told):
+        @pl.when(summing)
+        def _():
+            if heard is not None:
+                pl.semaphore_wait(round_sem.at[heard], len(next_chips))
+            if told is not None:
+                for peer in next_chips:
+                    pl.semaphore_signal(round_sem.at[told], inc=1, device_id=peer, device_id_type=MESH)
+
     def count(flag):
         return flag.astype(jnp.int32)
 
@@ -169,10 +185,10 @@
 
     @pl.when(summing)
     def _():
-        greet(plane_peers + z_peers)
+        greet(next_chips)
 
     n_greeted = (
-        2 + count(summing) * (len(plane_peers) + len(z_peers)) + 3 * count(crossing) + count(by_x) + 2 * count(by_z)
+        2 + count(summing) * len(next_chips) + 3 * count(crossing) + count(by_x) + 2 * count(by_z)
     )
 
     def mine(k):
@@ -409,7 +425,10 @@
         if levels == 0:
             pl.when(crossing)(exchange)
         if levels == EXCHANGE_AT:
-            pl.when(jnp.logical_not(crossing))(exchange)
+            pl.when(jnp.logical_not(jnp.logical_or(crossing, relaying)))(exchange)
+        if levels == 3:
+            pl.when(relaying)(exchange)
+            pass_on(None, 0)
 
     first = 3 * DEPTH
 
@@ -431,6 +450,7 @@
         return carry
 
     lax.fori_loop(first, rows + DEPTH, inner, 0)
+    pass_on(0, 1)
 
     decode_side(0)
     for i in range(DEPTH):
@@ -443,6 +463,7 @@
         return carry
 
     lax.fori_loop(0, DEPTH, near, 0)
+    pass_on(1, 2)
 
     decode_side(1)
 
@@ -453,6 +474,7 @@
         return carry
 
     lax.fori_loop(rows + DEPTH, total, far, 0)
+    pass_on(2, None)
     multiply(total - DEPTH - 1)
 
     whole = jnp.concatenate([acc[32 * b : 32 * b + 16, :] + acc[32 * b + 16 : 32 * b + 32, :] for b in range(4)], axis=0)
@@ -592,6 +614,7 @@
                 pltpu.SemaphoreType.DMA((2, DEPTH)),
                 pltpu.SemaphoreType.DMA((2, DEPTH)),
                 pltpu.SemaphoreType.DMA((4, 2)),
+                pltpu.SemaphoreType.REGULAR((3,)),
                 pltpu.SemaphoreType.DMA((n_red,)),
                 pltpu.SemaphoreType.DMA((n_red,)),
             ],

time: 42.8 us -> 42.7 us (level)
  no operation moved by 1% of the time
where the time goes in v3:
time: 42.7 us; the launch traced here: 42.6 us
  Pallas kernels  41 us (96%)
  local copies, waits for them, and re-layouts  1.57 us (4%)
    pallas_call x1, Pallas kernels, shards(): pl.pallas_call(functools.partial(kernel, dims), out_shape=jax.ShapeDtypeS...  41 us
    unnamed x1, local copies, waits for them, and re-layouts  1.57 us

profile of v3, /device:TPU:1, one launch (start us, length us, event | category | flops | bytes accessed | tf_op | source)
XLA Modules:
  0.0 42.6 jit_solution(13104098653366193273)
XLA Ops:
  0.0 41.0 %shard_map.55 = f32[4,4,16,16]{3,2,1,0:T(8,128)} custom-call(s32[16,16,2048]{2,1,0:T(8,128)} %signs.1, s32[16,2048]{1,0:T(8,128)} %disorder.1, s32[2,16,2048]{2,1,0:T(8,128)} %bonds.1, f32[8]{0:T(128)} %onsite_table.1, f32[4]{0:T(128)} %hop_table.1), custom_call_target="tpu_custom_call" | custom-call | tf_op jit(solution)/shard_map/pallas_call | solution.py:581
  41.0 1.6 %copy.7 = f32[4,4,16,16]{3,2,1,0:T(8,128)} copy(f32[4,4,16,16]{3,2,1,0:T(8,128)} %shard_map.55) | data formatting | bytes 32768
